TPU v7x, 256 devices: a whole 4x4x8 slice. The times are simulated.
256 devices in a mesh: seq: 32 (over y, z_lo, x), exp: 8 (over z_hi, core).
Axes of the slice: x: 4, y: 4, z: 8 (z_hi: 4, z_lo: 2; z = z_hi * 2 + z_lo), core: 2. Of those that a mesh axis runs over, the one named last changes fastest.
Arguments:
- query_input: bfloat16 [4096, 2048], P('seq', 'exp'), may hold values from -4.5 to 4.5
- key_input: bfloat16 [4096, 2048], P('seq', 'exp'), may hold values from -4.5 to 4.5
- value_input: bfloat16 [4096, 2048], P('seq', 'exp'), may hold values from -6 to 6
- segment_ids: int32 [4096], P('seq'), may hold values from 0 to 15, never falling along the last dimension, each value on 1 to 512 neighbouring positions
- residual_in: bfloat16 [4096, 4096], P('seq', 'exp'), may hold values from -13.5 to 13.5
- out_weight: bfloat16 [2048, 4096], P('exp'), may hold values from -0.1875 to 0.1875
- norm_gain: float32 [4096], P('exp'), may hold values from 0.1 to 1.9
- router: bfloat16 [4096, 32], P(None, 'seq'), may hold values from -0.1875 to 0.1875
- modality: int32 [4096], P('seq'), may hold values from 0 to 1
- expert_in: int32 [4096], P('seq'), may hold values from 0 to 15, as said below
- gate_weight: bfloat16 [32, 4096, 2816], P('seq', None, 'exp'), may hold values from -0.09375 to 0.09375
- up_weight: bfloat16 [32, 4096, 2816], P('seq', None, 'exp'), may hold values from -0.09375 to 0.09375
- down_weight: bfloat16 [32, 2816, 4096], P('seq', 'exp'), may hold values from -0.15625 to 0.15625
Outputs:
- layer_out: bfloat16 [4096, 4096], P('seq', 'exp')
Inputs may be any that keep to these rules, and one draw needn't show every extreme that they name: `segment_ids`: document numbers never fall along the sequence, and a document holds at most an eighth of the 4096 tokens. `expert_in`: within each aligned block of 128 tokens no expert (modality and number together) is chosen by more than 7 tokens, and in every block some expert is chosen by exactly 7.
All inputs are finite; a program needn't handle non-finite values.
Results may differ from a plain program's by a relative error of at most 0.0095.
Values may be sent and summed in bfloat16 or wider, within the bound.
A program may use at most 64 MiB of HBM per device.

v0:
```python
import jax
import jax.numpy as jnp
from jax import lax
from jax.sharding import Mesh
from jax.sharding import PartitionSpec as P

D = 4096
HEAD_DIM = 128
EXPERTS = 32
MODAL_EXPERTS = 16
CAPACITY = 7
EXP = ("exp_0", "exp_1")
NEGATIVE = -1e30
EPSILON = 1e-05


def passed_along(value, axis, steps):
    count = lax.axis_size(axis)
    leading, last = (max(0, -steps), min(count, count - steps))
    return lax.ppermute(value, axis, [(source, source + steps) for source in range(leading, last)])


def split_up(array, dim, length):
    lengths = array.shape
    tiles = array.reshape(*lengths[:dim], length, lengths[dim] // length, *lengths[dim + 1 :])
    return jnp.moveaxis(tiles, dim, 0)


def sent_and_summed(array, axis, dim):
    length = lax.axis_size(axis)
    tiles = lax.all_to_all(split_up(array, dim, length), axis, 0, 0, tiled=True)
    return jnp.sum(tiles.astype(jnp.float32), axis=0)


def copy_for_each(array, axis):
    copies = jnp.broadcast_to(array, (lax.axis_size(axis), *array.shape))
    return lax.all_to_all(copies, axis, split_axis=0, concat_axis=0, tiled=True)


def over_copies(array, axis):
    everything = copy_for_each(array, axis)
    return jnp.sum(everything, axis=0)


def joined_along(tiles, dim):
    tiles = jnp.moveaxis(tiles, 0, dim)
    lengths = tiles.shape
    return tiles.reshape(*lengths[:dim], lengths[dim] * lengths[dim + 1], *lengths[dim + 2 :])


def stacked_from(array, axes, turns):
    tiles = array
    for k in turns:
        tiles = lax.all_gather(tiles, axes[k])
    done = turns[::-1]
    back = [done.index(k) for k in range(len(axes))]
    tiles = tiles.transpose(*back, *range(len(axes), tiles.ndim))
    return tiles.reshape(-1, *array.shape)


def gather_axes(array, axes, turns, dim):
    return joined_along(stacked_from(array, axes, turns), dim)


def absorb(carry_state, query_heads, key_block, value_block, allowed):
    running_max, denominators, numerators = carry_state
    scores = jnp.einsum(
        "qhd,khd->hqk", query_heads, key_block, preferred_element_type=jnp.float32
    ) * HEAD_DIM ** (-0.5)
    masked = jnp.where(allowed[None], scores, NEGATIVE)
    new_max = jnp.maximum(running_max, jnp.max(masked, axis=2))
    rescale = jnp.exp(running_max - new_max)
    weights = jnp.exp(masked - new_max[:, :, None])
    denominators = denominators * rescale + jnp.sum(weights, axis=2)
    numerators = numerators * rescale[:, :, None] + jnp.einsum(
        "hqk,khd->hqd",
        weights.astype(jnp.bfloat16),
        value_block,
        preferred_element_type=jnp.float32,
    )
    return (new_max, denominators, numerators)


def local(
    query_input,
    key_input,
    value_input,
    segment_ids,
    residual_in,
    out_weight,
    norm_gain,
    router,
    modality,
    expert_in,
    gate_weight,
    up_weight,
    down_weight,
):
    token_count = query_input.shape[0]
    head_count = query_input.shape[1] // HEAD_DIM
    query_heads = query_input.reshape(token_count, head_count, HEAD_DIM)
    key_heads = key_input.reshape(token_count, head_count, HEAD_DIM)
    value_heads = value_input.reshape(token_count, head_count, HEAD_DIM)
    positions = jnp.arange(token_count, dtype=jnp.int32)
    local_mask = (segment_ids[:, None] == segment_ids[None, :]) & (
        positions[None, :] <= positions[:, None]
    )
    empty_state = (
        jnp.full((head_count, token_count), NEGATIVE, jnp.float32),
        jnp.zeros((head_count, token_count), jnp.float32),
        jnp.zeros((head_count, token_count, HEAD_DIM), jnp.float32),
    )
    carry_state = absorb(empty_state, query_heads, key_heads, value_heads, local_mask)
    cycle_index = lax.axis_index("seq")

    def visit(step_number, loop_carry):
        visit_state, key_block, value_block, travel_segments = loop_carry
        key_block, value_block, travel_segments = passed_along(
            (key_block, value_block, travel_segments), "seq", 1
        )
        has_block = cycle_index - step_number - 1 >= 0
        allowed = has_block & (segment_ids[:, None] == travel_segments.astype(jnp.int32)[None, :])
        visit_state = absorb(visit_state, query_heads, key_block, value_block, allowed)
        return (visit_state, key_block, value_block, travel_segments)

    start_carry = (carry_state, key_heads, value_heads, segment_ids.astype(jnp.bfloat16))
    final_carry = lax.fori_loop(0, lax.axis_size("seq") // 8, visit, start_carry)
    running_max, denominators, numerators = final_carry[0]
    attended = (numerators / denominators[:, :, None]).astype(jnp.bfloat16)
    attended = jnp.transpose(attended, (1, 0, 2)).reshape(token_count, head_count * HEAD_DIM)
    projected = jnp.dot(attended, out_weight, preferred_element_type=jnp.float32)
    attention = sent_and_summed(projected.astype(jnp.bfloat16), EXP, 1)
    residual = residual_in.astype(jnp.float32) + attention
    squares = jnp.sum(residual * residual, axis=1)
    square_total = over_copies(squares, EXP)
    normed = (residual * lax.rsqrt(square_total / D + EPSILON)[:, None] * norm_gain).astype(
        jnp.bfloat16
    )
    picked = modality * MODAL_EXPERTS + expert_in
    one_hot = (picked[:, None] == jnp.arange(EXPERTS, dtype=jnp.int32)[None, :]).astype(jnp.int32)
    rank_in_block = jnp.sum(one_hot * (jnp.cumsum(one_hot, axis=0) - 1), axis=1)
    slot_index = picked * CAPACITY + rank_in_block
    outgoing = (
        jnp.zeros((EXPERTS * CAPACITY, normed.shape[1]), jnp.bfloat16).at[slot_index].set(normed)
    )
    sliced = lax.all_to_all(
        outgoing.reshape(EXPERTS, CAPACITY, normed.shape[1]),
        "seq",
        split_axis=0,
        concat_axis=1,
        tiled=True,
    )
    arrived = gather_axes(sliced, EXP, (0, 1), 2)
    gate_sum = jnp.einsum("erd,edf->erf", arrived, gate_weight, preferred_element_type=jnp.float32)
    up_sum = jnp.einsum("erd,edf->erf", arrived, up_weight, preferred_element_type=jnp.float32)
    logits = jnp.einsum("erd,de->er", arrived, router, preferred_element_type=jnp.float32)
    hidden = (jax.nn.silu(gate_sum) * up_sum * jax.nn.sigmoid(logits)[:, :, None]).astype(
        jnp.bfloat16
    )
    partial_value = jnp.einsum(
        "erf,efd->erd", hidden, down_weight, preferred_element_type=jnp.float32
    )
    summed = lax.psum_scatter(
        partial_value.astype(jnp.bfloat16), EXP, scatter_dimension=2, tiled=True
    )
    returned = lax.all_to_all(summed, "seq", split_axis=1, concat_axis=0, tiled=True)
    routed = returned.reshape(EXPERTS * CAPACITY, returned.shape[2])[slot_index]
    return (residual + routed.astype(jnp.float32)).astype(jnp.bfloat16)


def solution(mesh):
    split = Mesh(mesh.devices.reshape(mesh.shape["seq"], 4, 2), ("seq", "exp_0", "exp_1"))
    placed = (
        P("seq", EXP),
        P("seq", EXP),
        P("seq", EXP),
        P("seq"),
        P("seq", EXP),
        P(EXP, None),
        P(EXP),
        P(None, "seq"),
        P("seq"),
        P("seq"),
        P("seq", None, EXP),
        P("seq", None, EXP),
        P("seq", EXP, None),
    )
    return jax.shard_map(
        local, mesh=split, in_specs=placed, out_specs=P("seq", EXP), check_vma=False
    )
```

profile of v0, /device:TPU:2, one launch (start us, length us, event | category | flops | bytes accessed | tf_op | source)
XLA Modules:
  0.0 265.8 jit_solution(9415738646136405745)
XLA Ops:
  6.5 0.9 fusion.41
  7.4 0.7 convert_element_type.62
  8.1 0.9 copy.78
  9.1 1.0 copy.79
  10.3 0.2 fusion.44
  10.6 1.0 copy.82
  11.7 0.2 convolution_add_fusion.1
  11.9 56.5 %while.25 = (s32[]{:T(128)}, f32[2,128]{1,0:T(2,128)S(1)}, f32[2,128]{1,0:T(2,128)S(1)}, f32[2,128,128]{2,1,0:T(8,128)S(1)}, bf16[128,2,128]{2,0,1:T(8,128)(2,1)...) while((s32[]{:T(128)}, f32[2,128]{1,0:T(2,128)S(1)}, ...), condition=%wide.region_5.6_spmd, body=%wide.region_2.5_spmd.sunk | while | flops 17171076 | bytes 1723927 | solution.py:127
  11.9 3.4 %collective-permute-start = (bf16[128]{0:T(256)(128)(2,1)S(1)}, bf16[128]{0:T(256)(128)(2,1)S(1)}, u32[]{:S(2)}, u32[]{:S(2)}) collective-permute-start(bf16[128]{0:T(256)(128)(2,1)S(1)} %get-tuple-element.416), channel_id=1, source_target_pairs={{0,8},{8,16},{16,24},{24,32},{32,40},{40,48},{48,56},{56,64},{64,7... | collective-permute-start | bytes 776 | tf_op jit(solution)/shard_map/while/body/eval_jaxpr/ppermute | solution.py:20
  15.3 3.1 %collective-permute-start.1 = (bf16[128,2,128]{2,0,1:T(8,128)(2,1)S(1)}, bf16[128,2,128]{2,0,1:T(8,128)(2,1)S(1)}, u32[]{:S(2)}, u32[]{:S(2)}) collective-permute-start(bf16[128,2,128]{2,0,1:T(8,128)(2,1)S(1)} %get-tuple-element.414), channel_id=1, source_target_pairs={{0,8},{8,16},{16,24},{24,32},{32,40},{40,48},{48,56},{56,64},{64,7... | collective-permute-start | bytes 196616 | tf_op jit(solution)/shard_map/while/body/eval_jaxpr/ppermute | solution.py:20
  18.5 3.7 %collective-permute-start.2 = (bf16[128,2,128]{2,0,1:T(8,128)(2,1)S(1)}, bf16[128,2,128]{2,0,1:T(8,128)(2,1)S(1)}, u32[]{:S(2)}, u32[]{:S(2)}) collective-permute-start(bf16[128,2,128]{2,0,1:T(8,128)(2,1)S(1)} %get-tuple-element.415), channel_id=1, source_target_pairs={{0,8},{8,16},{16,24},{24,32},{32,40},{40,48},{48,56},{56,64},{64,7... | collective-permute-start | bytes 196616 | tf_op jit(solution)/shard_map/while/body/eval_jaxpr/ppermute | solution.py:20
  22.2 0.7 compare_and_fusion.2
  23.0 0.2 select_reduce_fusion.3
  23.3 1.3 collective-permute-done.2
  24.6 0.2 convolution_add_fusion.3
  24.9 3.7 %collective-permute-start = (bf16[128]{0:T(256)(128)(2,1)S(1)}, bf16[128]{0:T(256)(128)(2,1)S(1)}, u32[]{:S(2)}, u32[]{:S(2)}) collective-permute-start(bf16[128]{0:T(256)(128)(2,1)S(1)} %get-tuple-element.416), channel_id=1, source_target_pairs={{0,8},{8,16},{16,24},{24,32},{32,40},{40,48},{48,56},{56,64},{64,7... | collective-permute-start | bytes 776 | tf_op jit(solution)/shard_map/while/body/eval_jaxpr/ppermute | solution.py:20
  28.6 3.4 %collective-permute-start.1 = (bf16[128,2,128]{2,0,1:T(8,128)(2,1)S(1)}, bf16[128,2,128]{2,0,1:T(8,128)(2,1)S(1)}, u32[]{:S(2)}, u32[]{:S(2)}) collective-permute-start(bf16[128,2,128]{2,0,1:T(8,128)(2,1)S(1)} %get-tuple-element.414), channel_id=1, source_target_pairs={{0,8},{8,16},{16,24},{24,32},{32,40},{40,48},{48,56},{56,64},{64,7... | collective-permute-start | bytes 196616 | tf_op jit(solution)/shard_map/while/body/eval_jaxpr/ppermute | solution.py:20
  32.0 5.5 %collective-permute-start.2 = (bf16[128,2,128]{2,0,1:T(8,128)(2,1)S(1)}, bf16[128,2,128]{2,0,1:T(8,128)(2,1)S(1)}, u32[]{:S(2)}, u32[]{:S(2)}) collective-permute-start(bf16[128,2,128]{2,0,1:T(8,128)(2,1)S(1)} %get-tuple-element.415), channel_id=1, source_target_pairs={{0,8},{8,16},{16,24},{24,32},{32,40},{40,48},{48,56},{56,64},{64,7... | collective-permute-start | bytes 196616 | tf_op jit(solution)/shard_map/while/body/eval_jaxpr/ppermute | solution.py:20
  37.6 0.7 compare_and_fusion.2
  38.7 0.8 collective-permute-done.2
  39.5 0.2 convolution_add_fusion.3
  39.7 4.3 %collective-permute-start = (bf16[128]{0:T(256)(128)(2,1)S(1)}, bf16[128]{0:T(256)(128)(2,1)S(1)}, u32[]{:S(2)}, u32[]{:S(2)}) collective-permute-start(bf16[128]{0:T(256)(128)(2,1)S(1)} %get-tuple-element.416), channel_id=1, source_target_pairs={{0,8},{8,16},{16,24},{24,32},{32,40},{40,48},{48,56},{56,64},{64,7... | collective-permute-start | bytes 776 | tf_op jit(solution)/shard_map/while/body/eval_jaxpr/ppermute | solution.py:20
  44.0 1.9 collective-permute-start.1
  45.9 4.1 %collective-permute-start.2 = (bf16[128,2,128]{2,0,1:T(8,128)(2,1)S(1)}, bf16[128,2,128]{2,0,1:T(8,128)(2,1)S(1)}, u32[]{:S(2)}, u32[]{:S(2)}) collective-permute-start(bf16[128,2,128]{2,0,1:T(8,128)(2,1)S(1)} %get-tuple-element.415), channel_id=1, source_target_pairs={{0,8},{8,16},{16,24},{24,32},{32,40},{40,48},{48,56},{56,64},{64,7... | collective-permute-start | bytes 196616 | tf_op jit(solution)/shard_map/while/body/eval_jaxpr/ppermute | solution.py:20
  50.1 0.7 compare_and_fusion.2
  51.2 0.9 collective-permute-done.2
  52.1 0.2 convolution_add_fusion.3
  52.4 4.1 %collective-permute-start = (bf16[128]{0:T(256)(128)(2,1)S(1)}, bf16[128]{0:T(256)(128)(2,1)S(1)}, u32[]{:S(2)}, u32[]{:S(2)}) collective-permute-start(bf16[128]{0:T(256)(128)(2,1)S(1)} %get-tuple-element.416), channel_id=1, source_target_pairs={{0,8},{8,16},{16,24},{24,32},{32,40},{40,48},{48,56},{56,64},{64,7... | collective-permute-start | bytes 776 | tf_op jit(solution)/shard_map/while/body/eval_jaxpr/ppermute | solution.py:20
  56.5 3.4 %collective-permute-start.1 = (bf16[128,2,128]{2,0,1:T(8,128)(2,1)S(1)}, bf16[128,2,128]{2,0,1:T(8,128)(2,1)S(1)}, u32[]{:S(2)}, u32[]{:S(2)}) collective-permute-start(bf16[128,2,128]{2,0,1:T(8,128)(2,1)S(1)} %get-tuple-element.414), channel_id=1, source_target_pairs={{0,8},{8,16},{16,24},{24,32},{32,40},{40,48},{48,56},{56,64},{64,7... | collective-permute-start | bytes 196616 | tf_op jit(solution)/shard_map/while/body/eval_jaxpr/ppermute | solution.py:20
  59.9 6.4 %collective-permute-start.2 = (bf16[128,2,128]{2,0,1:T(8,128)(2,1)S(1)}, bf16[128,2,128]{2,0,1:T(8,128)(2,1)S(1)}, u32[]{:S(2)}, u32[]{:S(2)}) collective-permute-start(bf16[128,2,128]{2,0,1:T(8,128)(2,1)S(1)} %get-tuple-element.415), channel_id=1, source_target_pairs={{0,8},{8,16},{16,24},{24,32},{32,40},{40,48},{48,56},{56,64},{64,7... | collective-permute-start | bytes 196616 | tf_op jit(solution)/shard_map/while/body/eval_jaxpr/ppermute | solution.py:20
  66.3 0.7 compare_and_fusion.2
  67.4 0.8 collective-permute-done.2
  68.2 0.2 convolution_add_fusion.3
  68.6 2.1 convolution_convert_fusion.1
  70.7 1.1 copy.106
  71.8 8.6 %all-to-all-start = ((bf16[8,128,512]{2,1,0:T(8,128)(2,1)}), bf16[8,128,512]{2,1,0:T(8,128)(2,1)}, u32[]{:S(2)}, u32[]{:S(2)}) async-start(bf16[8,128,512]{2,1,0:T(8,128)(2,1)} %bitcast.76), calls=%async_computation | async-start | bytes 2097152 | tf_op jit(solution)/shard_map/all_to_all | solution.py:31
  80.9 28.9 %all-to-all-done = bf16[8,128,512]{2,1,0:T(8,128)(2,1)} async-done(((bf16[8,128,512]{2,1,0:T(8,128)(2,1)}), bf16[8,128,512]{2,1,0:T(8,128)(2,1)}, u32[]{:S(2)}, u32[]{:S(2)}) %all-to-all-start) | async-done | bytes 1048608 | tf_op jit(solution)/shard_map/all_to_all | solution.py:31
  109.8 1.4 convert_reduce_fusion
  111.3 0.6 broadcast_in_dim.92
  111.9 3.3 %all-to-all-start.1 = ((f32[8,1,128]{2,1,0:T(1,128)}), f32[8,1,128]{2,1,0:T(1,128)S(1)}, u32[]{:S(2)}, u32[]{:S(2)}) async-start(f32[8,1,128]{2,1,0:T(1,128)} %broadcast_in_dim.92), calls=%async_computation.1 | async-start | bytes 8192 | tf_op jit(solution)/shard_map/all_to_all | solution.py:37
  115.3 7.5 %all-to-all-done.1 = f32[8,1,128]{2,1,0:T(1,128)S(1)} async-done(((f32[8,1,128]{2,1,0:T(1,128)}), f32[8,1,128]{2,1,0:T(1,128)S(1)}, u32[]{:S(2)}, u32[]{:S(2)}) %all-to-all-start.1) | async-done | bytes 4128 | tf_op jit(solution)/shard_map/all_to_all | solution.py:37
  122.8 1.2 scatter_custom_fusion
  124.0 0.8 reshape.170
  124.8 16.9 %all_to_all.29 = bf16[32,7,512]{2,1,0:T(8,128)(2,1)} all-to-all(bf16[32,7,512]{2,1,0:T(8,128)(2,1)} %reshape.170), channel_id=1, replica_groups=mesh['seq'=32,'exp_0'=4,'exp_1'=2] {'seq'}, dimensions={0} | all-to-all | bytes 458752 | tf_op jit(solution)/shard_map/all_to_all | solution.py:146
  141.6 1.0 all_gather.12
  142.7 20.1 %all_gather.13 = bf16[4,1,224,512]{3,2,1,0:T(8,128)(2,1)} all-gather(bf16[1,1,224,512]{3,2,1,0:T(8,128)(2,1)S(1)} %all_gather.12), channel_id=1, replica_groups=mesh['seq'=32,'exp_0'=4,'exp_1'=2] {'exp_0'}, dimensions={0}, use_global_device_ids=true | all-gather | bytes 1146880 | tf_op jit(solution)/shard_map/all_gather | solution.py:54
  162.8 12.2 %all-gather.3.cloned.1.call-done = bf16[8,1,224,512]{3,2,1,0:T(8,128)(2,1)} async-done(((bf16[4,1,224,512]{3,2,1,0:T(8,128)(2,1)}), bf16[8,1,224,512]{3,2,1,0:T(8,128)(2,1)}) %all-gather.3.cloned.1.call-update) | async-done | bytes 1835024 | tf_op jit(solution)/shard_map/all_gather | solution.py:54
  175.0 1.7 copy.91
  176.7 0.2 copy.101
  177.0 2.2 copy-done.5
  179.2 1.9 fusion.11
  181.1 0.6 fusion.45
  181.7 6.1 %fusion.7 = bf16[1,224,4096]{2,1,0:T(8,128)(2,1)} fusion(bf16[1,352,4096]{2,1,0:T(8,128)(2,1)S(1)} %copy-done, bf16[224,4096]{1,0:T(8,128)(2,1)} %bitcast.72, bf16[1,4096,352]{1,2,0:T(8,128)(2,1)} %param.26, f32[224,352]{1,0:T(8,128)} %fusion.11, f32[224]{0:T(256)S(1)} %add_divide_fusion), kind=kOutput, calls=%fused_computation.16 | convolution fusion | flops 1293315072 | bytes 9753472 | tf_op jit(solution)/shard_map/erf,efd->erd/dot_general | solution.py:160
  187.9 44.3 %reduce-scatter.2.cloned.1.call-done = bf16[1,224,512]{2,1,0:T(8,128)(2,1)} async-done(((bf16[1,224,4096]{2,1,0:T(8,128)(2,1)}), bf16[1,224,512]{2,1,0:T(8,128)(2,1)}) %reduce-scatter.2.cloned.1.call-update) | async-done | bytes 229392 | tf_op jit(solution)/shard_map/reduce_scatter | solution.py:163
  232.1 2.1 copy.108
  234.2 0.5 broadcast.146
  234.7 2.9 %reduce.1 = bf16[224,512]{1,0:T(8,128)(2,1)S(1)} reduce(bf16[224,1,512]{2,1,0:T(2,128)(2,1)} %bitcast.78, bf16[]{:T(256)} %broadcast.146), dimensions={1}, to_apply=%bitcast.63.reduce_sub_computation | reduce | bytes 458754
  237.6 0.8 reshape.202
  238.4 7.4 %all-to-all-start.3 = ((bf16[32,2,1792]{2,1,0:T(2,128)(2,1)}), bf16[32,2,1792]{2,1,0:T(2,128)(2,1)S(1)}, u32[]{:S(2)}, u32[]{:S(2)}) async-start(bf16[32,2,1792]{2,1,0:T(2,128)(2,1)} %reshape.202), calls=%async_computation.4 | async-start | bytes 458752 | tf_op jit(solution)/shard_map/all_to_all | solution.py:166
  245.9 8.0 %all-to-all-done.3 = bf16[32,2,1792]{2,1,0:T(2,128)(2,1)S(1)} async-done(((bf16[32,2,1792]{2,1,0:T(2,128)(2,1)}), bf16[32,2,1792]{2,1,0:T(2,128)(2,1)S(1)}, u32[]{:S(2)}, u32[]{:S(2)}) %all-to-all-start.3) | async-done | bytes 229408 | tf_op jit(solution)/shard_map/all_to_all | solution.py:166
  253.9 0.9 reshape.203
  254.8 1.1 copy.107
  255.9 1.5 gather_fusion
  257.4 1.6 add_convert_fusion
  (80 shorter events, 2.3 us)
Async XLA Ops:
  6.5 175.2 %copy-start = (bf16[1,352,4096]{2,1,0:T(8,128)(2,1)S(1)}, bf16[1,352,4096]{2,1,0:T(8,128)(2,1)}, u32[]{:S(2)}) copy-start(bf16[1,352,4096]{2,1,0:T(8,128)(2,1)} %param.27) | copy-start | bytes 8650756
  11.9 10.3 %collective-permute-start = (bf16[128]{0:T(256)(128)(2,1)S(1)}, bf16[128]{0:T(256)(128)(2,1)S(1)}, u32[]{:S(2)}, u32[]{:S(2)}) collective-permute-start(bf16[128]{0:T(256)(128)(2,1)S(1)} %get-tuple-element.416), channel_id=1, source_target_pairs={{0,8},{8,16},{16,24},{24,32},{32,40},{40,48},{48,56},{56,64},{64,7... | collective-permute-start | bytes 776 | tf_op jit(solution)/shard_map/while/body/eval_jaxpr/ppermute | solution.py:20
  15.3 7.7 %collective-permute-start.1 = (bf16[128,2,128]{2,0,1:T(8,128)(2,1)S(1)}, bf16[128,2,128]{2,0,1:T(8,128)(2,1)S(1)}, u32[]{:S(2)}, u32[]{:S(2)}) collective-permute-start(bf16[128,2,128]{2,0,1:T(8,128)(2,1)S(1)} %get-tuple-element.414), channel_id=1, source_target_pairs={{0,8},{8,16},{16,24},{24,32},{32,40},{40,48},{48,56},{56,64},{64,7... | collective-permute-start | bytes 196616 | tf_op jit(solution)/shard_map/while/body/eval_jaxpr/ppermute | solution.py:20
  18.5 6.2 %collective-permute-start.2 = (bf16[128,2,128]{2,0,1:T(8,128)(2,1)S(1)}, bf16[128,2,128]{2,0,1:T(8,128)(2,1)S(1)}, u32[]{:S(2)}, u32[]{:S(2)}) collective-permute-start(bf16[128,2,128]{2,0,1:T(8,128)(2,1)S(1)} %get-tuple-element.415), channel_id=1, source_target_pairs={{0,8},{8,16},{16,24},{24,32},{32,40},{40,48},{48,56},{56,64},{64,7... | collective-permute-start | bytes 196616 | tf_op jit(solution)/shard_map/while/body/eval_jaxpr/ppermute | solution.py:20
  24.9 12.7 %collective-permute-start = (bf16[128]{0:T(256)(128)(2,1)S(1)}, bf16[128]{0:T(256)(128)(2,1)S(1)}, u32[]{:S(2)}, u32[]{:S(2)}) collective-permute-start(bf16[128]{0:T(256)(128)(2,1)S(1)} %get-tuple-element.416), channel_id=1, source_target_pairs={{0,8},{8,16},{16,24},{24,32},{32,40},{40,48},{48,56},{56,64},{64,7... | collective-permute-start | bytes 776 | tf_op jit(solution)/shard_map/while/body/eval_jaxpr/ppermute | solution.py:20
  28.6 9.7 %collective-permute-start.1 = (bf16[128,2,128]{2,0,1:T(8,128)(2,1)S(1)}, bf16[128,2,128]{2,0,1:T(8,128)(2,1)S(1)}, u32[]{:S(2)}, u32[]{:S(2)}) collective-permute-start(bf16[128,2,128]{2,0,1:T(8,128)(2,1)S(1)} %get-tuple-element.414), channel_id=1, source_target_pairs={{0,8},{8,16},{16,24},{24,32},{32,40},{40,48},{48,56},{56,64},{64,7... | collective-permute-start | bytes 196616 | tf_op jit(solution)/shard_map/while/body/eval_jaxpr/ppermute | solution.py:20
  32.0 7.4 %collective-permute-start.2 = (bf16[128,2,128]{2,0,1:T(8,128)(2,1)S(1)}, bf16[128,2,128]{2,0,1:T(8,128)(2,1)S(1)}, u32[]{:S(2)}, u32[]{:S(2)}) collective-permute-start(bf16[128,2,128]{2,0,1:T(8,128)(2,1)S(1)} %get-tuple-element.415), channel_id=1, source_target_pairs={{0,8},{8,16},{16,24},{24,32},{32,40},{40,48},{48,56},{56,64},{64,7... | collective-permute-start | bytes 196616 | tf_op jit(solution)/shard_map/while/body/eval_jaxpr/ppermute | solution.py:20
  39.7 10.4 %collective-permute-start = (bf16[128]{0:T(256)(128)(2,1)S(1)}, bf16[128]{0:T(256)(128)(2,1)S(1)}, u32[]{:S(2)}, u32[]{:S(2)}) collective-permute-start(bf16[128]{0:T(256)(128)(2,1)S(1)} %get-tuple-element.416), channel_id=1, source_target_pairs={{0,8},{8,16},{16,24},{24,32},{32,40},{40,48},{48,56},{56,64},{64,7... | collective-permute-start | bytes 776 | tf_op jit(solution)/shard_map/while/body/eval_jaxpr/ppermute | solution.py:20
  44.0 6.9 %collective-permute-start.1 = (bf16[128,2,128]{2,0,1:T(8,128)(2,1)S(1)}, bf16[128,2,128]{2,0,1:T(8,128)(2,1)S(1)}, u32[]{:S(2)}, u32[]{:S(2)}) collective-permute-start(bf16[128,2,128]{2,0,1:T(8,128)(2,1)S(1)} %get-tuple-element.414), channel_id=1, source_target_pairs={{0,8},{8,16},{16,24},{24,32},{32,40},{40,48},{48,56},{56,64},{64,7... | collective-permute-start | bytes 196616 | tf_op jit(solution)/shard_map/while/body/eval_jaxpr/ppermute | solution.py:20
  45.9 6.2 %collective-permute-start.2 = (bf16[128,2,128]{2,0,1:T(8,128)(2,1)S(1)}, bf16[128,2,128]{2,0,1:T(8,128)(2,1)S(1)}, u32[]{:S(2)}, u32[]{:S(2)}) collective-permute-start(bf16[128,2,128]{2,0,1:T(8,128)(2,1)S(1)} %get-tuple-element.415), channel_id=1, source_target_pairs={{0,8},{8,16},{16,24},{24,32},{32,40},{40,48},{48,56},{56,64},{64,7... | collective-permute-start | bytes 196616 | tf_op jit(solution)/shard_map/while/body/eval_jaxpr/ppermute | solution.py:20
  52.4 14.0 %collective-permute-start = (bf16[128]{0:T(256)(128)(2,1)S(1)}, bf16[128]{0:T(256)(128)(2,1)S(1)}, u32[]{:S(2)}, u32[]{:S(2)}) collective-permute-start(bf16[128]{0:T(256)(128)(2,1)S(1)} %get-tuple-element.416), channel_id=1, source_target_pairs={{0,8},{8,16},{16,24},{24,32},{32,40},{40,48},{48,56},{56,64},{64,7... | collective-permute-start | bytes 776 | tf_op jit(solution)/shard_map/while/body/eval_jaxpr/ppermute | solution.py:20
  56.5 10.6 %collective-permute-start.1 = (bf16[128,2,128]{2,0,1:T(8,128)(2,1)S(1)}, bf16[128,2,128]{2,0,1:T(8,128)(2,1)S(1)}, u32[]{:S(2)}, u32[]{:S(2)}) collective-permute-start(bf16[128,2,128]{2,0,1:T(8,128)(2,1)S(1)} %get-tuple-element.414), channel_id=1, source_target_pairs={{0,8},{8,16},{16,24},{24,32},{32,40},{40,48},{48,56},{56,64},{64,7... | collective-permute-start | bytes 196616 | tf_op jit(solution)/shard_map/while/body/eval_jaxpr/ppermute | solution.py:20
  59.9 8.3 %collective-permute-start.2 = (bf16[128,2,128]{2,0,1:T(8,128)(2,1)S(1)}, bf16[128,2,128]{2,0,1:T(8,128)(2,1)S(1)}, u32[]{:S(2)}, u32[]{:S(2)}) collective-permute-start(bf16[128,2,128]{2,0,1:T(8,128)(2,1)S(1)} %get-tuple-element.415), channel_id=1, source_target_pairs={{0,8},{8,16},{16,24},{24,32},{32,40},{40,48},{48,56},{56,64},{64,7... | collective-permute-start | bytes 196616 | tf_op jit(solution)/shard_map/while/body/eval_jaxpr/ppermute | solution.py:20
  70.7 9.8 %copy-start.6 = (s32[128]{0:T(128)S(1)}, s32[128]{0:T(128)}, u32[]{:S(2)}) copy-start(s32[128]{0:T(128)} %param.24) | copy-start | bytes 1540
  70.7 9.8 %copy-start.7 = (s32[128]{0:T(128)S(1)}, s32[128]{0:T(128)}, u32[]{:S(2)}) copy-start(s32[128]{0:T(128)} %param.23) | copy-start | bytes 1540
  71.8 39.3 %copy-start.2 = (bf16[128,512]{1,0:T(8,128)(2,1)S(1)}, bf16[128,512]{1,0:T(8,128)(2,1)}, u32[]{:S(2)}) copy-start(bf16[128,512]{1,0:T(8,128)(2,1)} %param.19) | copy-start | bytes 393220
  71.8 51.0 %copy-start.4 = (f32[512]{0:T(512)S(1)}, f32[512]{0:T(512)}, u32[]{:S(2)}) copy-start(f32[512]{0:T(512)} %param.21) | copy-start | bytes 6148
  71.8 37.9 %all-to-all-start = ((bf16[8,128,512]{2,1,0:T(8,128)(2,1)}), bf16[8,128,512]{2,1,0:T(8,128)(2,1)}, u32[]{:S(2)}, u32[]{:S(2)}) async-start(bf16[8,128,512]{2,1,0:T(8,128)(2,1)} %bitcast.76), calls=%async_computation | async-start | bytes 2097152 | tf_op jit(solution)/shard_map/all_to_all | solution.py:31
  111.9 10.9 %all-to-all-start.1 = ((f32[8,1,128]{2,1,0:T(1,128)}), f32[8,1,128]{2,1,0:T(1,128)S(1)}, u32[]{:S(2)}, u32[]{:S(2)}) async-start(f32[8,1,128]{2,1,0:T(1,128)} %broadcast_in_dim.92), calls=%async_computation.1 | async-start | bytes 8192 | tf_op jit(solution)/shard_map/all_to_all | solution.py:37
  115.2 59.8 %all-gather.3.cloned.1.call-start = ((), (), s32[]{:S(2)}) async-start(), calls=%async_computation.6 | async-start | bytes 2752512 | tf_op jit(solution)/shard_map/all_gather | solution.py:54
  162.8 69.4 %reduce-scatter.2.cloned.1.call-start = ((), (), s32[]{:S(2)}) async-start(), calls=%async_computation.5 | async-start | bytes 2064384 | tf_op jit(solution)/shard_map/reduce_scatter | solution.py:163
  176.7 2.5 copy-start.5
  177.0 4.2 %copy-start.1 = (bf16[28,8,8,512]{3,1,2,0:T(8,128)(2,1)}, bf16[28,8,8,512]{3,1,2,0:T(8,128)(2,1)S(1)}, u32[]{:S(2)}) copy-start(bf16[28,8,8,512]{3,1,2,0:T(8,128)(2,1)S(1)} %copy.101) | copy-start | bytes 5505028
  179.2 1.9 copy-start.3
  238.4 15.5 %all-to-all-start.3 = ((bf16[32,2,1792]{2,1,0:T(2,128)(2,1)}), bf16[32,2,1792]{2,1,0:T(2,128)(2,1)S(1)}, u32[]{:S(2)}, u32[]{:S(2)}) async-start(bf16[32,2,1792]{2,1,0:T(2,128)(2,1)} %reshape.202), calls=%async_computation.4 | async-start | bytes 458752 | tf_op jit(solution)/shard_map/all_to_all | solution.py:166
Sparse Core Ops, SparseCore 0:
  162.9 12.1 all-gather.2
  188.0 44.1 reduce-scatter.1
where the time goes:
time: 267 us; the launch traced here: 266 us
  waiting for transfers between devices  105 us (39%)
  starting transfers between devices  66.5 us (25%)
  blocking collectives  36.9 us (14%)
  local copies, waits for them, and re-layouts  18 us (7%)
  between operations  13.7 us (5%)
  matrix products  12.9 us (5%)
  other arithmetic  12.6 us (5%)
    ppermute x12, starting transfers between devices, passed_along(): lax.ppermute(value, axis, [(source, source + steps) for source in range(l...  47.2 us
    reduce_scatter x1, waiting for transfers between devices, local(): lax.psum_scatter(partial_value.astype(jnp.bfloat16), EXP, scatter_dimensi...  44.3 us
    all_to_all x1, waiting for transfers between devices, sent_and_summed(): tiles = lax.all_to_all(split_up(array, dim, length), axis, 0, 0, tiled=True)  28.9 us
    all_gather x1, blocking collectives, stacked_from(): tiles = lax.all_gather(tiles, axes[k])  20.1 us
    all_to_all x1, blocking collectives, local(): lax.all_to_all(outgoing.reshape(EXPERTS, CAPACITY, normed.shape[1]), 'seq...  16.9 us
    all_gather x1, waiting for transfers between devices, stacked_from(): tiles = lax.all_gather(tiles, axes[k])  12.2 us
    unnamed x24, local copies, waits for them, and re-layouts  8.64 us
    all_to_all x1, starting transfers between devices, sent_and_summed(): tiles = lax.all_to_all(split_up(array, dim, length), axis, 0, 0, tiled=True)  8.59 us
  transfers between devices with their start and end apart: 17, of which 9 were waited for; matrix products, arithmetic and copies ran while one was open for 2% of the time, Pallas kernels for 0%

commit v1 on v0

--- a/solution.py
+++ b/solution.py
@@ -143,12 +143,20 @@
     outgoing = (
         jnp.zeros((EXPERTS * CAPACITY, normed.shape[1]), jnp.bfloat16).at[slot_index].set(normed)
     )
-    sliced = lax.all_to_all(
-        outgoing.reshape(EXPERTS, CAPACITY, normed.shape[1]),
-        "seq",
-        split_axis=0,
-        concat_axis=1,
-        tiled=True,
+    sliced = jnp.concatenate(
+        lax.all_to_all(
+            jnp.stack(
+                jnp.split(
+                    outgoing.reshape(EXPERTS, CAPACITY, normed.shape[1]),
+                    lax.axis_size("seq"),
+                    axis=0,
+                )
+            ),
+            "seq",
+            0,
+            0,
+        ),
+        axis=1,
     )
     arrived = gather_axes(sliced, EXP, (0, 1), 2)
     gate_sum = jnp.einsum("erd,edf->erf", arrived, gate_weight, preferred_element_type=jnp.float32)

time: 267 us -> 266 us (level)
    unnamed x24 -> x55, local copies, waits for them, and re-layouts: 8.64 us -> 8.85 us
where the time goes in v1:
time: 266 us; the launch traced here: 265 us
  waiting for transfers between devices  105 us (39%)
  starting transfers between devices  66.6 us (25%)
  blocking collectives  36.7 us (14%)
  local copies, waits for them, and re-layouts  17.4 us (7%)
  between operations  13.9 us (5%)
  matrix products  12.9 us (5%)
  other arithmetic  12.6 us (5%)
    ppermute x12, starting transfers between devices, passed_along(): lax.ppermute(value, axis, [(source, source + steps) for source in range(l...  47.2 us
    reduce_scatter x1, waiting for transfers between devices, local(): lax.psum_scatter(partial_value.astype(jnp.bfloat16), EXP, scatter_dimensi...  44.3 us
    all_to_all x1, waiting for transfers between devices, sent_and_summed(): tiles = lax.all_to_all(split_up(array, dim, length), axis, 0, 0, tiled=True)  28.9 us
    all_gather x1, blocking collectives, stacked_from(): tiles = lax.all_gather(tiles, axes[k])  20.1 us
    all_to_all x1, blocking collectives, local(): lax.all_to_all(jnp.stack(jnp.split(outgoing.reshape(EXPERTS, CAPACITY, no...  16.7 us
    all_gather x1, waiting for transfers between devices, stacked_from(): tiles = lax.all_gather(tiles, axes[k])  12.2 us
    unnamed x55, local copies, waits for them, and re-layouts  8.85 us
    all_to_all x1, starting transfers between devices, sent_and_summed(): tiles = lax.all_to_all(split_up(array, dim, length), axis, 0, 0, tiled=True)  8.59 us
  transfers between devices with their start and end apart: 17, of which 9 were waited for; matrix products, arithmetic and copies ran while one was open for 2% of the time, Pallas kernels for 0%

profile of v1, /device:TPU:2, one launch (start us, length us, event | category | flops | bytes accessed | tf_op | source)
XLA Modules:
  0.0 265.3 jit_solution(10153336820321099183)
XLA Ops:
  6.5 0.9 fusion.41
  7.4 0.7 convert_element_type.62
  8.1 0.9 copy.109
  9.1 1.0 copy.110
  10.3 0.2 fusion.44
  10.6 1.0 copy.113
  11.7 0.2 convolution_add_fusion.1
  11.9 56.5 %while.25 = (s32[]{:T(128)}, f32[2,128]{1,0:T(2,128)S(1)}, f32[2,128]{1,0:T(2,128)S(1)}, f32[2,128,128]{2,1,0:T(8,128)S(1)}, bf16[128,2,128]{2,0,1:T(8,128)(2,1)...) while((s32[]{:T(128)}, f32[2,128]{1,0:T(2,128)S(1)}, ...), condition=%wide.region_5.6_spmd, body=%wide.region_2.5_spmd.sunk | while | flops 17171076 | bytes 1723927 | solution.py:127
  11.9 3.4 %collective-permute-start = (bf16[128]{0:T(256)(128)(2,1)S(1)}, bf16[128]{0:T(256)(128)(2,1)S(1)}, u32[]{:S(2)}, u32[]{:S(2)}) collective-permute-start(bf16[128]{0:T(256)(128)(2,1)S(1)} %get-tuple-element.416), channel_id=1, source_target_pairs={{0,8},{8,16},{16,24},{24,32},{32,40},{40,48},{48,56},{56,64},{64,7... | collective-permute-start | bytes 776 | tf_op jit(solution)/shard_map/while/body/eval_jaxpr/ppermute | solution.py:20
  15.3 3.1 %collective-permute-start.1 = (bf16[128,2,128]{2,0,1:T(8,128)(2,1)S(1)}, bf16[128,2,128]{2,0,1:T(8,128)(2,1)S(1)}, u32[]{:S(2)}, u32[]{:S(2)}) collective-permute-start(bf16[128,2,128]{2,0,1:T(8,128)(2,1)S(1)} %get-tuple-element.414), channel_id=1, source_target_pairs={{0,8},{8,16},{16,24},{24,32},{32,40},{40,48},{48,56},{56,64},{64,7... | collective-permute-start | bytes 196616 | tf_op jit(solution)/shard_map/while/body/eval_jaxpr/ppermute | solution.py:20
  18.5 3.7 %collective-permute-start.2 = (bf16[128,2,128]{2,0,1:T(8,128)(2,1)S(1)}, bf16[128,2,128]{2,0,1:T(8,128)(2,1)S(1)}, u32[]{:S(2)}, u32[]{:S(2)}) collective-permute-start(bf16[128,2,128]{2,0,1:T(8,128)(2,1)S(1)} %get-tuple-element.415), channel_id=1, source_target_pairs={{0,8},{8,16},{16,24},{24,32},{32,40},{40,48},{48,56},{56,64},{64,7... | collective-permute-start | bytes 196616 | tf_op jit(solution)/shard_map/while/body/eval_jaxpr/ppermute | solution.py:20
  22.2 0.7 compare_and_fusion.2
  23.0 0.2 select_reduce_fusion.3
  23.3 1.3 collective-permute-done.2
  24.6 0.2 convolution_add_fusion.3
  24.9 3.7 %collective-permute-start = (bf16[128]{0:T(256)(128)(2,1)S(1)}, bf16[128]{0:T(256)(128)(2,1)S(1)}, u32[]{:S(2)}, u32[]{:S(2)}) collective-permute-start(bf16[128]{0:T(256)(128)(2,1)S(1)} %get-tuple-element.416), channel_id=1, source_target_pairs={{0,8},{8,16},{16,24},{24,32},{32,40},{40,48},{48,56},{56,64},{64,7... | collective-permute-start | bytes 776 | tf_op jit(solution)/shard_map/while/body/eval_jaxpr/ppermute | solution.py:20
  28.6 3.4 %collective-permute-start.1 = (bf16[128,2,128]{2,0,1:T(8,128)(2,1)S(1)}, bf16[128,2,128]{2,0,1:T(8,128)(2,1)S(1)}, u32[]{:S(2)}, u32[]{:S(2)}) collective-permute-start(bf16[128,2,128]{2,0,1:T(8,128)(2,1)S(1)} %get-tuple-element.414), channel_id=1, source_target_pairs={{0,8},{8,16},{16,24},{24,32},{32,40},{40,48},{48,56},{56,64},{64,7... | collective-permute-start | bytes 196616 | tf_op jit(solution)/shard_map/while/body/eval_jaxpr/ppermute | solution.py:20
  32.0 5.5 %collective-permute-start.2 = (bf16[128,2,128]{2,0,1:T(8,128)(2,1)S(1)}, bf16[128,2,128]{2,0,1:T(8,128)(2,1)S(1)}, u32[]{:S(2)}, u32[]{:S(2)}) collective-permute-start(bf16[128,2,128]{2,0,1:T(8,128)(2,1)S(1)} %get-tuple-element.415), channel_id=1, source_target_pairs={{0,8},{8,16},{16,24},{24,32},{32,40},{40,48},{48,56},{56,64},{64,7... | collective-permute-start | bytes 196616 | tf_op jit(solution)/shard_map/while/body/eval_jaxpr/ppermute | solution.py:20
  37.6 0.7 compare_and_fusion.2
  38.7 0.8 collective-permute-done.2
  39.5 0.2 convolution_add_fusion.3
  39.7 4.3 %collective-permute-start = (bf16[128]{0:T(256)(128)(2,1)S(1)}, bf16[128]{0:T(256)(128)(2,1)S(1)}, u32[]{:S(2)}, u32[]{:S(2)}) collective-permute-start(bf16[128]{0:T(256)(128)(2,1)S(1)} %get-tuple-element.416), channel_id=1, source_target_pairs={{0,8},{8,16},{16,24},{24,32},{32,40},{40,48},{48,56},{56,64},{64,7... | collective-permute-start | bytes 776 | tf_op jit(solution)/shard_map/while/body/eval_jaxpr/ppermute | solution.py:20
  44.0 1.9 collective-permute-start.1
  45.9 4.1 %collective-permute-start.2 = (bf16[128,2,128]{2,0,1:T(8,128)(2,1)S(1)}, bf16[128,2,128]{2,0,1:T(8,128)(2,1)S(1)}, u32[]{:S(2)}, u32[]{:S(2)}) collective-permute-start(bf16[128,2,128]{2,0,1:T(8,128)(2,1)S(1)} %get-tuple-element.415), channel_id=1, source_target_pairs={{0,8},{8,16},{16,24},{24,32},{32,40},{40,48},{48,56},{56,64},{64,7... | collective-permute-start | bytes 196616 | tf_op jit(solution)/shard_map/while/body/eval_jaxpr/ppermute | solution.py:20
  50.1 0.7 compare_and_fusion.2
  51.2 0.9 collective-permute-done.2
  52.1 0.2 convolution_add_fusion.3
  52.4 4.1 %collective-permute-start = (bf16[128]{0:T(256)(128)(2,1)S(1)}, bf16[128]{0:T(256)(128)(2,1)S(1)}, u32[]{:S(2)}, u32[]{:S(2)}) collective-permute-start(bf16[128]{0:T(256)(128)(2,1)S(1)} %get-tuple-element.416), channel_id=1, source_target_pairs={{0,8},{8,16},{16,24},{24,32},{32,40},{40,48},{48,56},{56,64},{64,7... | collective-permute-start | bytes 776 | tf_op jit(solution)/shard_map/while/body/eval_jaxpr/ppermute | solution.py:20
  56.5 3.4 %collective-permute-start.1 = (bf16[128,2,128]{2,0,1:T(8,128)(2,1)S(1)}, bf16[128,2,128]{2,0,1:T(8,128)(2,1)S(1)}, u32[]{:S(2)}, u32[]{:S(2)}) collective-permute-start(bf16[128,2,128]{2,0,1:T(8,128)(2,1)S(1)} %get-tuple-element.414), channel_id=1, source_target_pairs={{0,8},{8,16},{16,24},{24,32},{32,40},{40,48},{48,56},{56,64},{64,7... | collective-permute-start | bytes 196616 | tf_op jit(solution)/shard_map/while/body/eval_jaxpr/ppermute | solution.py:20
  59.9 6.4 %collective-permute-start.2 = (bf16[128,2,128]{2,0,1:T(8,128)(2,1)S(1)}, bf16[128,2,128]{2,0,1:T(8,128)(2,1)S(1)}, u32[]{:S(2)}, u32[]{:S(2)}) collective-permute-start(bf16[128,2,128]{2,0,1:T(8,128)(2,1)S(1)} %get-tuple-element.415), channel_id=1, source_target_pairs={{0,8},{8,16},{16,24},{24,32},{32,40},{40,48},{48,56},{56,64},{64,7... | collective-permute-start | bytes 196616 | tf_op jit(solution)/shard_map/while/body/eval_jaxpr/ppermute | solution.py:20
  66.3 0.7 compare_and_fusion.2
  67.1 0.2 select_reduce_fusion.3
  67.4 0.8 collective-permute-done.2
  68.2 0.2 convolution_add_fusion.3
  68.6 2.1 convolution_convert_fusion.1
  70.7 1.1 copy.137
  71.8 8.6 %all-to-all-start = ((bf16[8,128,512]{2,1,0:T(8,128)(2,1)}), bf16[8,128,512]{2,1,0:T(8,128)(2,1)}, u32[]{:S(2)}, u32[]{:S(2)}) async-start(bf16[8,128,512]{2,1,0:T(8,128)(2,1)} %bitcast.204), calls=%async_computation | async-start | bytes 2097152 | tf_op jit(solution)/shard_map/all_to_all | solution.py:31
  80.9 28.9 %all-to-all-done = bf16[8,128,512]{2,1,0:T(8,128)(2,1)} async-done(((bf16[8,128,512]{2,1,0:T(8,128)(2,1)}), bf16[8,128,512]{2,1,0:T(8,128)(2,1)}, u32[]{:S(2)}, u32[]{:S(2)}) %all-to-all-start) | async-done | bytes 1048608 | tf_op jit(solution)/shard_map/all_to_all | solution.py:31
  109.8 1.4 convert_reduce_fusion
  111.3 0.6 broadcast_in_dim.92
  111.9 3.3 %all-to-all-start.1 = ((f32[8,1,128]{2,1,0:T(1,128)}), f32[8,1,128]{2,1,0:T(1,128)S(1)}, u32[]{:S(2)}, u32[]{:S(2)}) async-start(f32[8,1,128]{2,1,0:T(1,128)} %broadcast_in_dim.92), calls=%async_computation.1 | async-start | bytes 8192 | tf_op jit(solution)/shard_map/all_to_all | solution.py:37
  115.3 7.5 %all-to-all-done.1 = f32[8,1,128]{2,1,0:T(1,128)S(1)} async-done(((f32[8,1,128]{2,1,0:T(1,128)}), f32[8,1,128]{2,1,0:T(1,128)S(1)}, u32[]{:S(2)}, u32[]{:S(2)}) %all-to-all-start.1) | async-done | bytes 4128 | tf_op jit(solution)/shard_map/all_to_all | solution.py:37
  122.8 1.2 scatter_custom_fusion
  124.4 16.7 %all_to_all.25 = bf16[32,1,7,512]{3,2,1,0:T(8,128)(2,1)} all-to-all(bf16[32,1,7,512]{3,2,1,0:T(8,128)(2,1)S(1)} %constant_dynamic-update-slice_fusion), channel_id=1, replica_groups=mesh['seq'=32,'exp_0'=4,'exp_1'=2] {'seq'}, dimensions={0} | all-to-all | bytes 458752 | tf_op jit(solution)/shard_map/all_to_all | solution.py:147
  141.1 1.0 all_gather_reshape.3
  142.2 20.1 %all_gather.9 = bf16[4,1,224,512]{3,2,1,0:T(8,128)(2,1)} all-gather(bf16[1,1,224,512]{3,2,1,0:T(8,128)(2,1)S(1)} %all_gather_reshape.3), channel_id=1, replica_groups=mesh['seq'=32,'exp_0'=4,'exp_1'=2] {'exp_0'}, dimensions={0}, use_global_device_ids=true | all-gather | bytes 1146880 | tf_op jit(solution)/shard_map/all_gather | solution.py:54
  162.3 12.2 %all-gather.3.cloned.1.call-done = bf16[8,1,224,512]{3,2,1,0:T(8,128)(2,1)} async-done(((bf16[4,1,224,512]{3,2,1,0:T(8,128)(2,1)}), bf16[8,1,224,512]{3,2,1,0:T(8,128)(2,1)}) %all-gather.3.cloned.1.call-update) | async-done | bytes 1835024 | tf_op jit(solution)/shard_map/all_gather | solution.py:54
  174.5 1.7 copy.122
  176.2 0.2 copy.132
  176.5 2.2 copy-done.5
  178.7 1.9 fusion.11
  180.6 0.6 fusion.45
  181.2 6.1 %fusion.7 = bf16[1,224,4096]{2,1,0:T(8,128)(2,1)} fusion(bf16[1,352,4096]{2,1,0:T(8,128)(2,1)S(1)} %copy-done, bf16[224,4096]{1,0:T(8,128)(2,1)} %bitcast.200, bf16[1,4096,352]{1,2,0:T(8,128)(2,1)} %param.26, f32[224,352]{1,0:T(8,128)} %fusion.11, f32[224]{0:T(256)S(1)} %add_divide_fusion), kind=kOutput, calls=%fused_computation.16 | convolution fusion | flops 1293315072 | bytes 9753472 | tf_op jit(solution)/shard_map/erf,efd->erd/dot_general | solution.py:168
  187.3 44.3 %reduce-scatter.2.cloned.1.call-done = bf16[1,224,512]{2,1,0:T(8,128)(2,1)} async-done(((bf16[1,224,4096]{2,1,0:T(8,128)(2,1)}), bf16[1,224,512]{2,1,0:T(8,128)(2,1)}) %reduce-scatter.2.cloned.1.call-update) | async-done | bytes 229392 | tf_op jit(solution)/shard_map/reduce_scatter | solution.py:171
  231.6 2.1 copy.139
  233.7 0.5 broadcast.146
  234.2 2.9 %reduce.1 = bf16[224,512]{1,0:T(8,128)(2,1)S(1)} reduce(bf16[224,1,512]{2,1,0:T(2,128)(2,1)} %bitcast.206, bf16[]{:T(256)} %broadcast.146), dimensions={1}, to_apply=%bitcast.191.reduce_sub_computation | reduce | bytes 458754
  237.1 0.8 reshape.259
  237.9 7.4 %all-to-all-start.3 = ((bf16[32,2,1792]{2,1,0:T(2,128)(2,1)}), bf16[32,2,1792]{2,1,0:T(2,128)(2,1)S(1)}, u32[]{:S(2)}, u32[]{:S(2)}) async-start(bf16[32,2,1792]{2,1,0:T(2,128)(2,1)} %reshape.259), calls=%async_computation.4 | async-start | bytes 458752 | tf_op jit(solution)/shard_map/all_to_all | solution.py:174
  245.4 8.0 %all-to-all-done.3 = bf16[32,2,1792]{2,1,0:T(2,128)(2,1)S(1)} async-done(((bf16[32,2,1792]{2,1,0:T(2,128)(2,1)}), bf16[32,2,1792]{2,1,0:T(2,128)(2,1)S(1)}, u32[]{:S(2)}, u32[]{:S(2)}) %all-to-all-start.3) | async-done | bytes 229408 | tf_op jit(solution)/shard_map/all_to_all | solution.py:174
  253.4 0.9 reshape.260
  254.3 1.1 copy.138
  255.4 1.5 gather_fusion
  256.9 1.6 add_convert_fusion
  (111 shorter events, 2.3 us)
Async XLA Ops:
  6.5 174.7 %copy-start = (bf16[1,352,4096]{2,1,0:T(8,128)(2,1)S(1)}, bf16[1,352,4096]{2,1,0:T(8,128)(2,1)}, u32[]{:S(2)}) copy-start(bf16[1,352,4096]{2,1,0:T(8,128)(2,1)} %param.27) | copy-start | bytes 8650756
  11.9 10.3 %collective-permute-start = (bf16[128]{0:T(256)(128)(2,1)S(1)}, bf16[128]{0:T(256)(128)(2,1)S(1)}, u32[]{:S(2)}, u32[]{:S(2)}) collective-permute-start(bf16[128]{0:T(256)(128)(2,1)S(1)} %get-tuple-element.416), channel_id=1, source_target_pairs={{0,8},{8,16},{16,24},{24,32},{32,40},{40,48},{48,56},{56,64},{64,7... | collective-permute-start | bytes 776 | tf_op jit(solution)/shard_map/while/body/eval_jaxpr/ppermute | solution.py:20
  15.3 7.7 %collective-permute-start.1 = (bf16[128,2,128]{2,0,1:T(8,128)(2,1)S(1)}, bf16[128,2,128]{2,0,1:T(8,128)(2,1)S(1)}, u32[]{:S(2)}, u32[]{:S(2)}) collective-permute-start(bf16[128,2,128]{2,0,1:T(8,128)(2,1)S(1)} %get-tuple-element.414), channel_id=1, source_target_pairs={{0,8},{8,16},{16,24},{24,32},{32,40},{40,48},{48,56},{56,64},{64,7... | collective-permute-start | bytes 196616 | tf_op jit(solution)/shard_map/while/body/eval_jaxpr/ppermute | solution.py:20
  18.5 6.2 %collective-permute-start.2 = (bf16[128,2,128]{2,0,1:T(8,128)(2,1)S(1)}, bf16[128,2,128]{2,0,1:T(8,128)(2,1)S(1)}, u32[]{:S(2)}, u32[]{:S(2)}) collective-permute-start(bf16[128,2,128]{2,0,1:T(8,128)(2,1)S(1)} %get-tuple-element.415), channel_id=1, source_target_pairs={{0,8},{8,16},{16,24},{24,32},{32,40},{40,48},{48,56},{56,64},{64,7... | collective-permute-start | bytes 196616 | tf_op jit(solution)/shard_map/while/body/eval_jaxpr/ppermute | solution.py:20
  24.9 12.7 %collective-permute-start = (bf16[128]{0:T(256)(128)(2,1)S(1)}, bf16[128]{0:T(256)(128)(2,1)S(1)}, u32[]{:S(2)}, u32[]{:S(2)}) collective-permute-start(bf16[128]{0:T(256)(128)(2,1)S(1)} %get-tuple-element.416), channel_id=1, source_target_pairs={{0,8},{8,16},{16,24},{24,32},{32,40},{40,48},{48,56},{56,64},{64,7... | collective-permute-start | bytes 776 | tf_op jit(solution)/shard_map/while/body/eval_jaxpr/ppermute | solution.py:20
  28.6 9.7 %collective-permute-start.1 = (bf16[128,2,128]{2,0,1:T(8,128)(2,1)S(1)}, bf16[128,2,128]{2,0,1:T(8,128)(2,1)S(1)}, u32[]{:S(2)}, u32[]{:S(2)}) collective-permute-start(bf16[128,2,128]{2,0,1:T(8,128)(2,1)S(1)} %get-tuple-element.414), channel_id=1, source_target_pairs={{0,8},{8,16},{16,24},{24,32},{32,40},{40,48},{48,56},{56,64},{64,7... | collective-permute-start | bytes 196616 | tf_op jit(solution)/shard_map/while/body/eval_jaxpr/ppermute | solution.py:20
  32.0 7.4 %collective-permute-start.2 = (bf16[128,2,128]{2,0,1:T(8,128)(2,1)S(1)}, bf16[128,2,128]{2,0,1:T(8,128)(2,1)S(1)}, u32[]{:S(2)}, u32[]{:S(2)}) collective-permute-start(bf16[128,2,128]{2,0,1:T(8,128)(2,1)S(1)} %get-tuple-element.415), channel_id=1, source_target_pairs={{0,8},{8,16},{16,24},{24,32},{32,40},{40,48},{48,56},{56,64},{64,7... | collective-permute-start | bytes 196616 | tf_op jit(solution)/shard_map/while/body/eval_jaxpr/ppermute | solution.py:20
  39.7 10.4 %collective-permute-start = (bf16[128]{0:T(256)(128)(2,1)S(1)}, bf16[128]{0:T(256)(128)(2,1)S(1)}, u32[]{:S(2)}, u32[]{:S(2)}) collective-permute-start(bf16[128]{0:T(256)(128)(2,1)S(1)} %get-tuple-element.416), channel_id=1, source_target_pairs={{0,8},{8,16},{16,24},{24,32},{32,40},{40,48},{48,56},{56,64},{64,7... | collective-permute-start | bytes 776 | tf_op jit(solution)/shard_map/while/body/eval_jaxpr/ppermute | solution.py:20
  44.0 6.9 %collective-permute-start.1 = (bf16[128,2,128]{2,0,1:T(8,128)(2,1)S(1)}, bf16[128,2,128]{2,0,1:T(8,128)(2,1)S(1)}, u32[]{:S(2)}, u32[]{:S(2)}) collective-permute-start(bf16[128,2,128]{2,0,1:T(8,128)(2,1)S(1)} %get-tuple-element.414), channel_id=1, source_target_pairs={{0,8},{8,16},{16,24},{24,32},{32,40},{40,48},{48,56},{56,64},{64,7... | collective-permute-start | bytes 196616 | tf_op jit(solution)/shard_map/while/body/eval_jaxpr/ppermute | solution.py:20
  45.9 6.2 %collective-permute-start.2 = (bf16[128,2,128]{2,0,1:T(8,128)(2,1)S(1)}, bf16[128,2,128]{2,0,1:T(8,128)(2,1)S(1)}, u32[]{:S(2)}, u32[]{:S(2)}) collective-permute-start(bf16[128,2,128]{2,0,1:T(8,128)(2,1)S(1)} %get-tuple-element.415), channel_id=1, source_target_pairs={{0,8},{8,16},{16,24},{24,32},{32,40},{40,48},{48,56},{56,64},{64,7... | collective-permute-start | bytes 196616 | tf_op jit(solution)/shard_map/while/body/eval_jaxpr/ppermute | solution.py:20
  52.4 14.0 %collective-permute-start = (bf16[128]{0:T(256)(128)(2,1)S(1)}, bf16[128]{0:T(256)(128)(2,1)S(1)}, u32[]{:S(2)}, u32[]{:S(2)}) collective-permute-start(bf16[128]{0:T(256)(128)(2,1)S(1)} %get-tuple-element.416), channel_id=1, source_target_pairs={{0,8},{8,16},{16,24},{24,32},{32,40},{40,48},{48,56},{56,64},{64,7... | collective-permute-start | bytes 776 | tf_op jit(solution)/shard_map/while/body/eval_jaxpr/ppermute | solution.py:20
  56.5 10.6 %collective-permute-start.1 = (bf16[128,2,128]{2,0,1:T(8,128)(2,1)S(1)}, bf16[128,2,128]{2,0,1:T(8,128)(2,1)S(1)}, u32[]{:S(2)}, u32[]{:S(2)}) collective-permute-start(bf16[128,2,128]{2,0,1:T(8,128)(2,1)S(1)} %get-tuple-element.414), channel_id=1, source_target_pairs={{0,8},{8,16},{16,24},{24,32},{32,40},{40,48},{48,56},{56,64},{64,7... | collective-permute-start | bytes 196616 | tf_op jit(solution)/shard_map/while/body/eval_jaxpr/ppermute | solution.py:20
  59.9 8.3 %collective-permute-start.2 = (bf16[128,2,128]{2,0,1:T(8,128)(2,1)S(1)}, bf16[128,2,128]{2,0,1:T(8,128)(2,1)S(1)}, u32[]{:S(2)}, u32[]{:S(2)}) collective-permute-start(bf16[128,2,128]{2,0,1:T(8,128)(2,1)S(1)} %get-tuple-element.415), channel_id=1, source_target_pairs={{0,8},{8,16},{16,24},{24,32},{32,40},{40,48},{48,56},{56,64},{64,7... | collective-permute-start | bytes 196616 | tf_op jit(solution)/shard_map/while/body/eval_jaxpr/ppermute | solution.py:20
  70.7 9.8 %copy-start.6 = (s32[128]{0:T(128)S(1)}, s32[128]{0:T(128)}, u32[]{:S(2)}) copy-start(s32[128]{0:T(128)} %param.24) | copy-start | bytes 1540
  70.7 9.8 %copy-start.7 = (s32[128]{0:T(128)S(1)}, s32[128]{0:T(128)}, u32[]{:S(2)}) copy-start(s32[128]{0:T(128)} %param.23) | copy-start | bytes 1540
  71.8 39.3 %copy-start.2 = (bf16[128,512]{1,0:T(8,128)(2,1)S(1)}, bf16[128,512]{1,0:T(8,128)(2,1)}, u32[]{:S(2)}) copy-start(bf16[128,512]{1,0:T(8,128)(2,1)} %param.19) | copy-start | bytes 393220
  71.8 51.0 %copy-start.4 = (f32[512]{0:T(512)S(1)}, f32[512]{0:T(512)}, u32[]{:S(2)}) copy-start(f32[512]{0:T(512)} %param.21) | copy-start | bytes 6148
  71.8 37.9 %all-to-all-start = ((bf16[8,128,512]{2,1,0:T(8,128)(2,1)}), bf16[8,128,512]{2,1,0:T(8,128)(2,1)}, u32[]{:S(2)}, u32[]{:S(2)}) async-start(bf16[8,128,512]{2,1,0:T(8,128)(2,1)} %bitcast.204), calls=%async_computation | async-start | bytes 2097152 | tf_op jit(solution)/shard_map/all_to_all | solution.py:31
  111.9 10.9 %all-to-all-start.1 = ((f32[8,1,128]{2,1,0:T(1,128)}), f32[8,1,128]{2,1,0:T(1,128)S(1)}, u32[]{:S(2)}, u32[]{:S(2)}) async-start(f32[8,1,128]{2,1,0:T(1,128)} %broadcast_in_dim.92), calls=%async_computation.1 | async-start | bytes 8192 | tf_op jit(solution)/shard_map/all_to_all | solution.py:37
  115.2 59.3 %all-gather.3.cloned.1.call-start = ((), (), s32[]{:S(2)}) async-start(), calls=%async_computation.6 | async-start | bytes 2752512 | tf_op jit(solution)/shard_map/all_gather | solution.py:54
  162.3 69.4 %reduce-scatter.2.cloned.1.call-start = ((), (), s32[]{:S(2)}) async-start(), calls=%async_computation.5 | async-start | bytes 2064384 | tf_op jit(solution)/shard_map/reduce_scatter | solution.py:171
  176.2 2.5 copy-start.5
  176.5 4.2 %copy-start.1 = (bf16[28,8,8,512]{3,1,2,0:T(8,128)(2,1)}, bf16[28,8,8,512]{3,1,2,0:T(8,128)(2,1)S(1)}, u32[]{:S(2)}) copy-start(bf16[28,8,8,512]{3,1,2,0:T(8,128)(2,1)S(1)} %copy.132) | copy-start | bytes 5505028
  178.7 1.9 copy-start.3
  237.9 15.5 %all-to-all-start.3 = ((bf16[32,2,1792]{2,1,0:T(2,128)(2,1)}), bf16[32,2,1792]{2,1,0:T(2,128)(2,1)S(1)}, u32[]{:S(2)}, u32[]{:S(2)}) async-start(bf16[32,2,1792]{2,1,0:T(2,128)(2,1)} %reshape.259), calls=%async_computation.4 | async-start | bytes 458752 | tf_op jit(solution)/shard_map/all_to_all | solution.py:174
Sparse Core Ops, SparseCore 0:
  162.4 12.1 all-gather.2
  187.5 44.1 reduce-scatter.1
